TPU v7x, 32 devices: a whole 2x2x4 slice. The times are simulated.
32 devices in a mesh: grp: 4 (over y, x), row: 8 (over z, core).
Axes of the slice: x: 2, y: 2, z: 4, core: 2. Of those that a mesh axis runs over, the one named last changes fastest.
Arguments:
- serving: bfloat16 [16384, 128], P('row'), may hold values from -1 to 1
- serving_scale: bfloat16 [128], P('row'), may hold values from 0.099609375 to 1
- hot_blocks: int32 [4, 16], P('grp', 'row'), may hold values from 0 to 15, as said below
- bag_lengths: int32 [32, 256], P(('grp', 'row')), may hold values from 1 to 16, 1024 in all within a row
- bag_indices: int32 [32, 1024], P(('grp', 'row')), may hold values from 0 to 2047, as said below
- dense_act: bfloat16 [8192, 128], P(('grp', 'row')), may hold values from -6 to 6
- labels: float32 [8192], P(('grp', 'row')), may hold values from 0 to 1
- w_top: bfloat16 [256, 1024], replicated, may hold values from -0.375 to 0.375
- w_out: float32 [1024], replicated, may hold values from -0.012 to 0.012
- master: float32 [4, 4096, 128], P('grp', 'row'), may hold values from -0.3 to 0.3
- accum: float32 [4, 4096], P('grp', 'row'), may hold values from 1e-05 to 0.0001
Outputs:
- new_master: float32 [4, 4096, 128], P('grp', 'row')
- new_accum: float32 [4, 4096], P('grp', 'row')
- new_serving: bfloat16 [16384, 128], P('row')
- new_scale: bfloat16 [128], P('row')
- top_grad: float32 [256, 1024], replicated
Inputs may be any that keep to these rules, and one draw needn't show every extreme that they name: `hot_blocks`: the 2 entries that one group names in one row shard are distinct. `bag_indices`: in each device's line, exactly 64 distinct values lie in each range of 256 consecutive positions that starts at a multiple of 256.
All inputs are finite; a program needn't handle non-finite values. Where the computation divides by a largest or mean magnitude, that divisor is 1e-20 or more.
Results may differ from a plain program's by a relative error of at most 0.012.
Values may be sent and summed in bfloat16 or wider, within the bound.
A program may use at most 128 MiB of HBM per device.

v0:
```python
import math

import jax
import jax.numpy as jnp
from jax import lax
from jax.sharding import PartitionSpec as P

BLOCK = 128
MOST = 16


lr_step = 0.05


def pool_grad(table, lengths, indices, dense_d, labels_d, w_top, w_out):
    rows, width = table.shape
    total = indices.shape[0]
    ends = jnp.cumsum(lengths)
    starts = ends - lengths
    slots = jnp.arange(MOST, dtype=jnp.int32)
    positions = jnp.minimum(starts[:, None] + slots[None, :], total - 1)
    picked = jnp.where(slots[None, :] < lengths[:, None], indices[positions], -1)
    span = math.gcd(rows, 2048)
    pieces = rows // span

    def count_block(first):
        columns = first + jnp.arange(span, dtype=jnp.int32)
        return jnp.sum((picked[:, :, None] == columns[None, None, :]).astype(jnp.bfloat16), axis=1)

    counts = lax.map(count_block, jnp.arange(pieces, dtype=jnp.int32) * span)
    table_blocks = table.reshape(pieces, span, width)

    def add_block(running, pair):
        block_counts, block_rows = pair
        return (
            running
            + jnp.dot(
                block_counts.astype(jnp.float32), block_rows, precision=lax.Precision.HIGHEST
            ),
            None,
        )

    pooled, _ = lax.scan(
        add_block, jnp.zeros((lengths.shape[0], width), jnp.float32), (counts, table_blocks)
    )
    joined = jnp.concatenate([pooled.astype(jnp.bfloat16), dense_d], axis=1)
    pre = jnp.dot(joined, w_top, preferred_element_type=jnp.float32)
    sig = jax.nn.sigmoid(pre)
    logit = jnp.dot(pre * sig, w_out, precision=lax.Precision.HIGHEST)
    dlogit = jax.nn.sigmoid(logit) - labels_d
    dpre = (dlogit[:, None] * w_out[None, :] * (sig * (1.0 + pre * (1.0 - sig)))).astype(
        jnp.bfloat16
    )
    top = lax.dot_general(
        joined, dpre, (((0,), (0,)), ((), ())), preferred_element_type=jnp.float32
    )
    dz = lax.dot_general(dpre, w_top, (((1,), (1,)), ((), ())), preferred_element_type=jnp.float32)
    emb_grad = dz[:, :width]

    def spread_block(block_counts):
        weights = block_counts.astype(jnp.float32)
        summed = lax.dot_general(
            weights, emb_grad, (((0,), (0,)), ((), ())), precision=lax.Precision.HIGHEST
        )
        return (summed, jnp.sum(weights, axis=0))

    hot, column_use = lax.map(spread_block, counts)
    return (top, hot.reshape(rows, width), column_use.reshape(rows) > 0)


def on_device(
    serving,
    serving_scale,
    hot_blocks,
    bag_lengths,
    bag_indices,
    dense_act,
    labels,
    w_top,
    w_out,
    master,
    accum,
):
    width = serving.shape[1]
    chosen = hot_blocks[0]
    count = chosen.shape[0]
    local_blocks = serving.reshape(-1, BLOCK, width)
    total_blocks = local_blocks.shape[0]
    picked = local_blocks[chosen]
    picked_scale = serving_scale[chosen]
    fetched, fetched_scale = (
        lax.all_gather(picked, "row", axis=0, tiled=True),
        lax.all_gather(picked_scale, "row", axis=0, tiled=True),
    )
    table = (
        fetched.astype(jnp.float32) * fetched_scale.astype(jnp.float32)[:, None, None]
    ).reshape(-1, width)
    top_part, hot_part, used_rows = pool_grad(
        table, bag_lengths[0], bag_indices[0], dense_act, labels, w_top, w_out
    )
    top_grad = lax.psum(top_part, ("grp", "row"))
    owned = lax.psum_scatter(hot_part, "row", scatter_dimension=0, tiled=True).reshape(
        count, BLOCK, width
    )
    quarter = lax.axis_index("grp")
    groups = lax.axis_size("grp")
    per_owner = total_blocks // groups
    arrived, arrived_ids = (
        lax.all_gather(owned, "grp", axis=0, tiled=True),
        lax.all_gather(chosen.astype(jnp.float32), "grp", axis=0, tiled=True),
    )
    slot = arrived_ids.astype(jnp.int32) - quarter * per_owner
    inside = (slot >= 0) & (slot < per_owner)
    slot = jnp.where(inside, slot, per_owner)
    grad = (
        jnp.zeros((per_owner, BLOCK, width), jnp.float32)
        .at[slot]
        .add(arrived, mode="drop")
        .reshape(-1, width)
    )
    weights = master[0]
    state = accum[0]
    new_state = state + jnp.mean(grad * grad, axis=1)
    new_weights = weights - lr_step * grad / jnp.sqrt(new_state)[:, None]
    scale_new = (
        jnp.max(jnp.abs(new_weights.reshape(per_owner, BLOCK * width)), axis=1) + 1e-06
    ).astype(jnp.bfloat16)
    coded = (
        (
            new_weights.reshape(per_owner, BLOCK, width)
            / scale_new.astype(jnp.float32)[:, None, None]
        )
        .astype(jnp.bfloat16)
        .reshape(-1, width)
    )
    fresh, fresh_scale = (
        lax.all_gather(coded, "grp", axis=0, tiled=True),
        lax.all_gather(scale_new, "grp", axis=0, tiled=True),
    )
    return (new_weights[None], new_state[None], fresh, fresh_scale, top_grad)


def solution(mesh):
    return jax.shard_map(
        on_device,
        mesh=mesh,
        in_specs=(
            P("row", None),
            P("row"),
            P("grp", "row"),
            P(("grp", "row"), None),
            P(("grp", "row"), None),
            P(("grp", "row"), None),
            P(("grp", "row")),
            P(),
            P(),
            P("grp", "row", None),
            P("grp", "row"),
        ),
        out_specs=(P("grp", "row", None), P("grp", "row"), P("row", None), P("row"), P()),
        check_vma=False,
    )
```

profile of v0, /device:TPU:1, one launch (start us, length us, event | category | flops | bytes accessed | tf_op | source)
XLA Modules:
  0.0 259.5 jit_solution(4268729098067179809)
XLA Ops:
  8.0 0.0 reduce-scatter.2.cloned.1.call-start
  8.1 1.0 reduce-window.9
  9.1 0.1 slice.10
  9.2 0.1 slice_reduce_fusion
  9.3 0.8 bitcast_subtract_fusion
  10.1 0.1 compare_select_fusion
  10.2 0.1 reshape.249
  10.4 16.7 %gather_fusion = s32[4096]{0:T(1024)S(1)} fusion(s32[1024]{0:T(1024)S(1)} %bitcast.46, s32[4096]{0:T(1024)S(1)} %broadcast_clamp_fusion), kind=kCustom, calls=%fused_computation | custom fusion | bytes 49152 | tf_op jit(solution)/shard_map/gather | solution.py:22
  27.1 0.1 reshape.248
  27.2 0.1 fusion.8
  27.3 0.6 dynamic-slice.2
  28.6 0.6 gather_fusion.2
  29.2 0.2 dynamic-update-slice.1
  29.5 10.4 %fusion.1 = bf16[256,2048]{1,0:T(8,128)(2,1)S(1)} fusion(s32[256,16]{1,0:T(8,128)S(1)} %fusion.8), kind=kLoop, calls=%fused_computation.6 | loop fusion | flops 24641536 | bytes 1064960 | tf_op jit(solution)/shard_map/while/body/eval_jaxpr/reduce_sum | solution.py:28
  39.9 14.6 %all-reduce.1 = bf16[16]{0:T(256)(128)(2,1)S(1)} all-reduce(bf16[16]{0:T(256)(128)(2,1)S(1)} %dynamic-update-slice.1), channel_id=4, replica_groups=mesh['grp'=4,'row'=8] {'row'}, use_global_device_ids=true, to_apply=%add.1 | all-reduce | flops 16 | bytes 64
  54.5 0.6 gather_fusion.1
  55.1 18.5 %all-gather.1 = bf16[16,128,128]{2,1,0:T(8,128)(2,1)S(1)} all-gather(bf16[2,128,128]{2,1,0:T(8,128)(2,1)S(1)} %gather_fusion.1), channel_id=3, replica_groups=mesh['grp'=4,'row'=8] {'row'}, dimensions={0}, use_global_device_ids=true | all-gather | bytes 589824 | tf_op jit(solution)/shard_map/all_gather | solution.py:92
  73.5 0.1 copy.19
  73.7 0.1 convert_multiply_fusion
  73.8 1.0 convolution_convert_fusion
  74.8 0.0 copy-done.3
  74.8 0.3 fusion.10
  75.2 0.4 copy-done.9
  75.5 1.1 fusion.2
  76.6 0.4 multiply_convert_fusion
  77.1 0.3 fusion.5
  77.4 2.2 fusion.18
  79.6 0.0 all-reduce.5.cloned.1.call-start
  79.6 0.6 copy-done.12
  80.2 0.6 dynamic-slice.1
  81.4 0.1 bitcast_dynamic-update-slice_fusion
  81.5 8.3 %all-reduce = f32[8]{0:T(128)S(1)} all-reduce(f32[8]{0:T(128)S(1)} %bitcast_dynamic-update-slice_fusion), channel_id=2, replica_groups=mesh['grp'=4,'row'=8] {'grp'}, use_global_device_ids=true, to_apply=%add | all-reduce | flops 8 | bytes 64
  90.5 1.3 fusion.9
  91.8 14.8 %reduce-scatter.2.cloned.1.call-done = f32[256,128]{1,0:T(8,128)} async-done(((f32[2048,128]{1,0:T(8,128)}), f32[256,128]{1,0:T(8,128)}) %reduce-scatter.2.cloned.1.call-update) | async-done | bytes 131088 | tf_op jit(solution)/shard_map/reduce_scatter | solution.py:102
  106.5 9.0 %all_gather.21 = f32[8,128,128]{2,1,0:T(8,128)S(1)} all-gather(f32[2,128,128]{2,1,0:T(8,128)} %bitcast.51), channel_id=1, replica_groups=mesh['grp'=4,'row'=8] {'grp'}, dimensions={0}, use_global_device_ids=true | all-gather | bytes 655360 | tf_op jit(solution)/shard_map/all_gather | solution.py:109
  115.6 1.0 scatter_fusion
  116.7 0.1 broadcast_multiply_fusion
  116.8 0.8 abs_reduce_fusion
  117.7 0.1 bitcast_reduce_fusion
  117.8 0.2 dynamic-update-slice.2
  118.1 7.4 %all-reduce.2 = bf16[16]{0:T(256)(128)(2,1)} all-reduce(bf16[16]{0:T(256)(128)(2,1)S(1)} %dynamic-update-slice.2), channel_id=1, replica_groups=mesh['grp'=4,'row'=8] {'grp'}, use_global_device_ids=true, to_apply=%add.2 | all-reduce | flops 16 | bytes 64
  125.5 0.2 divide_convert_fusion
  125.7 8.1 %all_gather.22 = bf16[2048,128]{1,0:T(8,128)(2,1)S(1)} all-gather(bf16[512,128]{1,0:T(8,128)(2,1)S(1)} %bitcast.50), channel_id=1, replica_groups=mesh['grp'=4,'row'=8] {'grp'}, dimensions={0}, use_global_device_ids=true | all-gather | bytes 655360 | tf_op jit(solution)/shard_map/all_gather | solution.py:137
  133.8 0.6 add.103
  134.4 115.3 %all-reduce.5.cloned.1.call-done = f32[256,1024]{1,0:T(8,128)} async-done(((f32[256,1024]{1,0:T(8,128)}), f32[256,1024]{1,0:T(8,128)}) %all-reduce.5.cloned.1.call-update) | async-done | bytes 1048592 | tf_op jit(solution)/shard_map/psum | solution.py:101
  249.7 0.8 copy.26
  250.5 0.6 copy-done.5
  251.1 1.0 copy.27
  (40 shorter events, 0.2 us)
Async XLA Ops:
  8.0 46.5 %copy-start = (bf16[2048,128]{1,0:T(8,128)(2,1)S(1)}, bf16[2048,128]{1,0:T(8,128)(2,1)}, u32[]{:S(2)}) copy-start(bf16[2048,128]{1,0:T(8,128)(2,1)} %param.11) | copy-start | bytes 1572868
  8.0 2.3 copy-start.1
  8.0 98.5 %reduce-scatter.2.cloned.1.call-start = ((), (), s32[]{:S(2)}) async-start(), calls=%async_computation.1 | async-start | bytes 1179648 | tf_op jit(solution)/shard_map/reduce_scatter | solution.py:102
  10.3 16.8 %copy-start.8 = (s32[1,256]{1,0:T(1,128)S(1)}, s32[1,256]{1,0:T(1,128)}, u32[]{:S(2)}) copy-start(s32[1,256]{1,0:T(1,128)} %param.14) | copy-start | bytes 3076
  10.3 16.9 %copy-start.11 = (s32[1,2]{1,0:T(1,128)S(1)}, s32[1,2]{1,0:T(1,128)}, u32[]{:S(2)}) copy-start(s32[1,2]{1,0:T(1,128)} %param.13) | copy-start | bytes 28
  10.3 17.0 %copy-start.13 = (u32[32]{0:T(128)S(1)}, u32[32]{0:T(128)}, u32[]{:S(2)}) copy-start(u32[32]{0:T(128)} %constant.82) | copy-start | bytes 388
  10.4 18.2 %copy-start.2 = (bf16[16]{0:T(256)(128)(2,1)S(1)}, bf16[16]{0:T(256)(128)(2,1)}, u32[]{:S(2)}) copy-start(bf16[16]{0:T(256)(128)(2,1)} %param.12) | copy-start | bytes 100
  29.2 44.3 %copy-start.6 = (bf16[256,128]{1,0:T(8,128)(2,1)S(1)}, bf16[256,128]{1,0:T(8,128)(2,1)}, u32[]{:S(2)}) copy-start(bf16[256,128]{1,0:T(8,128)(2,1)} %param.16) | copy-start | bytes 196612
  73.8 1.0 copy-start.3
  74.8 0.7 copy-start.9
  75.5 1.1 copy-start.10
  79.5 0.7 copy-start.12
  79.6 170.1 %all-reduce.5.cloned.1.call-start = ((), (), s32[]{:S(2)}) async-start(), calls=%async_computation.2 | async-start | bytes 2097152 | tf_op jit(solution)/shard_map/psum | solution.py:101
  115.6 1.2 copy-start.7
  115.6 1.2 copy-start.4
  249.7 1.4 copy-start.5
Sparse Core Ops, SparseCore 0:
  79.7 26.8 reduce-scatter.1
Sparse Core Ops, SparseCore 1:
  118.2 131.5 all-reduce.4
where the time goes:
time: 262 us; the launch traced here: 260 us
  waiting for transfers between devices  130 us (50%)
  blocking collectives  65.9 us (25%)
  local copies, waits for them, and re-layouts  23.5 us (9%)
  between operations  17.8 us (7%)
  other arithmetic  16 us (6%)
  matrix products  6.17 us (2%)
    psum x1, waiting for transfers between devices, on_device(): top_grad = lax.psum(top_part, ('grp', 'row'))  115 us
    unnamed x3, blocking collectives  30.3 us
    all_gather x1, blocking collectives, on_device(): lax.all_gather(picked, 'row', axis=0, tiled=True)  18.5 us
    gather x2, local copies, waits for them, and re-layouts, pool_grad(): indices[positions]  16.8 us
    reduce_scatter x1, waiting for transfers between devices, on_device(): lax.psum_scatter(hot_part, 'row', scatter_dimension=0, tiled=True)  14.8 us
    reduce_sum x1, other arithmetic, count_block(): jnp.sum((picked[:, :, None] == columns[None, None, :]).astype(jnp.bfloat1...  10.4 us
    all_gather x1, blocking collectives, on_device(): lax.all_gather(owned, 'grp', axis=0, tiled=True)  9.04 us
    all_gather x1, blocking collectives, on_device(): lax.all_gather(coded, 'grp', axis=0, tiled=True)  8.12 us
  transfers between devices with their start and end apart: 2, of which 2 were waited for; matrix products, arithmetic and copies ran while one was open for 1% of the time, Pallas kernels for 0%

commit v1 on v0

v1 whole, which is shorter than its diff:
```python
import functools

import jax
import jax.numpy as jnp
from jax import lax
from jax.experimental import pallas as pl
from jax.experimental.pallas import tpu as pltpu
from jax.sharding import PartitionSpec as P

BLOCK = 128
LR = 0.05
MESH = pl.DeviceIdType.MESH
BF = jnp.bfloat16
F32 = jnp.float32


def nt(a, b):
    return lax.dot_general(a, b, (((1,), (1,)), ((), ())), preferred_element_type=F32)


def nn(a, b):
    return jnp.dot(a, b, preferred_element_type=F32)


def tn(a, b):
    return lax.dot_general(a, b, (((0,), (0,)), ((), ())), preferred_element_type=F32)


def iota(shape, axis):
    return lax.broadcasted_iota(jnp.int32, shape, axis)


def to_column(row):
    m = row.shape[1]
    keep = iota((m, m), 0) == iota((m, m), 1)
    return jnp.sum(jnp.where(keep, row, jnp.zeros_like(row)), axis=1, keepdims=True)


def to_row(column):
    m = column.shape[0]
    keep = iota((m, m), 0) == iota((m, m), 1)
    return jnp.sum(jnp.where(keep, column, jnp.zeros_like(column)), axis=0, keepdims=True)


def rcopy(src, dst, send, recv, device):
    return pltpu.make_async_remote_copy(
        src_ref=src, dst_ref=dst, send_sem=send, recv_sem=recv,
        device_id=device, device_id_type=MESH,
    )


def loop(lo, hi, body):
    def step(k, carry):
        body(k)
        return carry

    lax.fori_loop(lo, hi, step, 0)


def kernel(
    dims,
    hot, srv, scl, lens, idx, dense, labels, w_top, w_out, master, accum,
    o_master, o_accum, o_srv, o_scl, o_top,
    tbl, cnt, cnt_t, sel, hmsg, hrecv, gbuf, sbuf, pooled, joined, dpre,
    t_send, t_own, t_a, t_b, t_br, t_c, t_cr, f_d, f_e, f_f,
    a_s, a_f, a_r, h_s, h_r, g_s, g_r, c_s, c_r, k_s, k_r,
    ta_s, ta_r, tb_s, tb_r, tc_s, tc_r, td_s, td_r, te_s, te_r, tf_s, tf_r,
):
    n, groups, cap = dims
    nz = n // 2
    g = lax.axis_index("grp")
    me = lax.axis_index("row")
    z, c = me // 2, me % 2
    pal = z * 2 + (1 - c)
    count = hot.shape[1]
    span = count * BLOCK
    capp = hmsg.shape[1] - 16
    bags = lens.shape[1]
    nnz = idx.shape[1]
    width = srv.shape[1]
    per = master.shape[0] // BLOCK
    ff = w_top.shape[1]
    half = ff // 2

    def row_peer(k):
        return (me + k) % n

    def chip_peer(k):
        return ((z + k) % nz) * 2 + c

    def grp_peer(k):
        return (g + k) % groups

    barrier = pltpu.get_barrier_semaphore()

    def greet(k):
        pl.semaphore_signal(barrier, inc=1, device_id=(g, row_peer(k)), device_id_type=MESH)

    loop(1, n, greet)
    for k in range(1, groups):
        pl.semaphore_signal(barrier, inc=1, device_id=(grp_peer(k), me), device_id_type=MESH)

    lane_b = iota((1, scl.shape[1]), 1)
    scales = scl[...].astype(F32)
    rows16 = iota((16, width), 0)
    scale_rows = jnp.zeros((16, width), F32)
    id_rows = jnp.zeros((16, width), F32)
    for j in range(count):
        block = hot[:, j:j + 1]
        one = jnp.sum(jnp.where(lane_b == block, scales, 0.0), axis=1, keepdims=True)
        scale_rows = jnp.where(rows16 == j, one, scale_rows)
        id_rows = jnp.where(rows16 == j, block.astype(F32), id_rows)
        chosen = jnp.broadcast_to(block, (8, width))
        rows = jnp.zeros((BLOCK, width), F32)
        for b in range(scl.shape[1]):
            mask = jnp.where(chosen == b, 1.0, 0.0)[0:1, :]
            rows = rows + srv[b * BLOCK:(b + 1) * BLOCK, :].astype(F32) * mask
        tbl[me, j * BLOCK:(j + 1) * BLOCK, :] = rows.astype(BF)
    tbl[me, span:span + 16, :] = scale_rows.astype(BF)
    gbuf[g, span:span + 16, :] = id_rows.astype(BF)

    pl.semaphore_wait(barrier, n - 1 + groups - 1)

    def a_copy(source, to, send):
        return rcopy(tbl.at[source], tbl.at[source], send, a_r.at[source], (g, to))

    loop(1, nz, lambda k: a_copy(me, chip_peer(k), a_s.at[k]).start())
    a_copy(me, pal, a_s.at[0]).start()

    lengths = lens[...]
    tri = iota((bags, bags), 1) <= iota((bags, bags), 0)
    ends = jnp.sum(jnp.where(tri, lengths, 0), axis=1, keepdims=True)
    starts = ends - to_column(lengths)
    place = iota((bags, nnz), 1)
    in_bag = jnp.where((place >= starts) & (place < ends), 1.0, 0.0).astype(BF)
    indices = idx[...]
    upper = jnp.where(iota((span, span), 0) <= iota((span, span), 1), 1.0, 0.0).astype(BF)
    numbers = iota((8, span), 1).astype(F32).astype(BF)

    def count_range(r):
        which = jnp.where(indices - r * span == iota((span, nnz), 0), 1.0, 0.0).astype(BF)
        cnt_t[r] = nt(which, in_bag).astype(BF)
        counts = nt(in_bag, which)
        cnt[r] = counts.astype(BF)
        used = jnp.where(jnp.sum(counts, axis=0, keepdims=True) > 0.0, 1.0, 0.0)
        rank = nn(jnp.broadcast_to(used, (8, span)).astype(BF), upper)[0:1, :]
        order = jnp.where(used > 0.0, rank.astype(jnp.int32) - 1, -1)
        picked = jnp.where(iota((width, span), 0) == order, 1.0, 0.0).astype(BF)
        sel[r] = picked[:capp, :]
        hmsg[r, capp:capp + 16, :] = jnp.concatenate(
            [nt(numbers, picked), jnp.zeros((8, width), F32)], axis=0
        ).astype(BF)

    loop(0, n, count_range)

    joined[:, width:] = dense[...]

    def relay(k):
        source = chip_peer(k)
        a_copy(source, source, a_f.at[k]).wait_recv()
        a_copy(source, pal, a_f.at[k]).start()

    loop(1, nz, relay)

    def other(k):
        source = ((z + k) % nz) * 2 + (1 - c)
        a_copy(source, pal, a_f.at[0]).wait_recv()

    loop(0, nz, other)
    pooled[...] = jnp.zeros_like(pooled)

    def pool(r):
        block_scale = tbl[r, span:span + 16, :].astype(F32)
        total = pooled[...]
        for j in range(count):
            part = slice(j * BLOCK, (j + 1) * BLOCK)
            total = total + nn(cnt[r, :, part], tbl[r, part, :]) * block_scale[j:j + 1, :]
        pooled[...] = total

    loop(0, n, pool)
    joined[:, :width] = pooled[...].astype(BF)

    pre = nn(joined[...], w_top[...])
    sig = jax.nn.sigmoid(pre)
    out_w = w_out[...]
    logit = jnp.sum(pre * sig * out_w, axis=1, keepdims=True)
    dlogit = jax.nn.sigmoid(logit) - to_column(labels[...])
    dp = (dlogit * out_w * (sig * (1.0 + pre * (1.0 - sig)))).astype(BF)
    dpre[0] = dp[:, :half]
    dpre[1] = dp[:, half:]
    dz = nt(dp, w_top[:width, :]).astype(BF)

    def h_copy(to, source, k):
        return rcopy(hmsg.at[to], hrecv.at[source], h_s.at[k], h_r.at[source], (g, to))

    def spread(k):
        to = row_peer(k)
        rows = nn(cnt_t[to], dz).astype(BF)
        hmsg[to, :capp, :] = nn(sel[to], rows).astype(BF)
        h_copy(to, me, k).start()

    loop(1, n, spread)

    def ta_copy():
        return rcopy(t_send, t_a, ta_s, ta_r, (g, pal))

    feats = w_top.shape[0]
    theirs = tn(joined[...], dpre[1 - c])
    for j in range(half // BLOCK):
        t_send[j * feats:(j + 1) * feats, :] = theirs[:, j * BLOCK:(j + 1) * BLOCK].astype(BF)
    ta_copy().start()
    mine = tn(joined[...], dpre[c])
    for j in range(half // BLOCK):
        t_own[j * feats:(j + 1) * feats, :] = mine[:, j * BLOCK:(j + 1) * BLOCK]

    pooled[...] = jnp.zeros_like(pooled)
    t_rows = nn(cnt_t[me], dz)

    def g_copy(k):
        return rcopy(gbuf.at[g], gbuf.at[g], g_s.at[k], g_r.at[k], (grp_peer(k), me))

    def arrive(k, total):
        source = row_peer(k)
        h_copy(source, source, k).wait_recv()
        place_of = hrecv[source, capp:capp + 1, :].astype(F32)
        put = jnp.where(
            iota((span, width), 0).astype(F32) == place_of, 1.0, 0.0
        ).astype(BF)
        return total + nn(put[:, :capp], hrecv[source, :capp, :])

    summed = lax.fori_loop(1, n, arrive, t_rows)
    gbuf[g, :span, :] = summed.astype(BF)
    for k in range(1, groups):
        g_copy(k).start()

    quarter = t_own.shape[0] // groups

    def part_of(ref, q):
        return ref.at[pl.ds(pl.multiple_of(q * quarter, quarter), quarter)]

    def tb_copy(k):
        return rcopy(
            part_of(t_b, grp_peer(k)), t_br.at[k], tb_s.at[k], tb_r.at[k], (grp_peer(k), me)
        )

    ta_copy().wait_recv()
    both = t_own[...] + t_a[...].astype(F32)
    t_own[...] = both
    t_b[...] = both.astype(BF)
    for k in range(1, groups):
        tb_copy(k).start()

    for k in range(1, groups):
        g_copy(k).wait_recv()
    srows = jnp.zeros((16, width), F32)
    quarter_at = (g * per).astype(F32)
    for b in range(per):
        grad = jnp.zeros((BLOCK, width), F32)
        for q in range(groups):
            for j in range(count):
                ids = gbuf[q, span:span + 16, :].astype(F32)[j:j + 1, :]
                grad = grad + jnp.where(
                    ids == quarter_at + b,
                    gbuf[q, j * BLOCK:(j + 1) * BLOCK, :].astype(F32),
                    0.0,
                )
        part = slice(b * BLOCK, (b + 1) * BLOCK)
        state = to_column(accum[:, part]) + jnp.sum(grad * grad, axis=1, keepdims=True) / width
        o_accum[:, part] = to_row(state)
        fresh = master[part, :] - LR * grad / jnp.sqrt(state)
        o_master[part, :] = fresh
        most = jnp.max(jnp.max(jnp.abs(fresh), axis=0, keepdims=True), axis=1, keepdims=True)
        scale = (most + 1e-6).astype(BF).astype(F32)
        o_srv[g, part, :] = (fresh / scale).astype(BF)
        srows = jnp.where(rows16 == b, scale, srows)
    sbuf[g] = srows.astype(BF)

    def c_copy(k):
        return rcopy(o_srv.at[g], o_srv.at[g], c_s.at[k], c_r.at[k], (grp_peer(k), me))

    def k_copy(k):
        return rcopy(sbuf.at[g], sbuf.at[g], k_s.at[k], k_r.at[k], (grp_peer(k), me))

    for k in range(1, groups):
        c_copy(k).start()
        k_copy(k).start()

    def tc_copy(k):
        to = chip_peer(k)
        return rcopy(t_c.at[to // 2], t_cr.at[k], tc_s.at[k], tc_r.at[k], (g, to))

    total = t_own[pl.ds(pl.multiple_of(g * quarter, quarter), quarter), :]
    for k in range(1, groups):
        tb_copy(k).wait_recv()
        total = total + t_br[k].astype(F32)
    piece = quarter // nz
    for q in range(nz):
        t_c[q] = total[q * piece:(q + 1) * piece, :].astype(t_c.dtype)
    loop(1, nz, lambda k: tc_copy(k).start())

    def gather_piece(k, total):
        tc_copy(k).wait_recv()
        return total + t_cr[k].astype(F32)

    final = lax.fori_loop(1, nz, gather_piece, t_c[z].astype(F32))

    def td_copy(k):
        return rcopy(f_d.at[z], f_d.at[z], td_s.at[k], td_r.at[k], (g, chip_peer(k)))

    f_d[z] = final.astype(BF).astype(f_d.dtype)
    loop(1, nz, lambda k: td_copy(k).start())
    loop(1, nz, lambda k: td_copy(k).wait_recv())

    def te_copy(k):
        return rcopy(f_e.at[g], f_e.at[g], te_s.at[k], te_r.at[k], (grp_peer(k), me))

    def tf_copy(k):
        q = grp_peer(k)
        return rcopy(f_e.at[q], f_f.at[q], tf_s.at[k], tf_r.at[k], (g, pal))

    f_e[g] = f_d[...].reshape(quarter, width).astype(BF)
    for k in range(1, groups):
        te_copy(k).start()
    tf_copy(0).start()
    for k in range(1, groups):
        te_copy(k).wait_recv()

    for k in range(1, groups):
        tf_copy(k).start()

    for k in range(1, groups):
        k_copy(k).wait_recv()
    lane = iota((1, width), 1)
    line = jnp.zeros((1, width), F32)
    for q in range(groups):
        block = sbuf[q].astype(F32)
        for b in range(per):
            line = jnp.where(lane == q * per + b, block[b:b + 1, :], line)
    o_scl[...] = line[:, :groups * per].astype(BF)

    def place_half(ref, at):
        flat = ref[...].reshape(groups * quarter, width).astype(F32)
        for j in range(half // BLOCK):
            column = pl.multiple_of(at * half + j * BLOCK, BLOCK)
            o_top[:, pl.ds(column, BLOCK)] = flat[j * feats:(j + 1) * feats, :]

    place_half(f_e, c)
    for k in range(groups):
        tf_copy(k).wait_recv()
    place_half(f_f, 1 - c)
    for k in range(1, groups):
        c_copy(k).wait_recv()

    a_copy(me, pal, a_s.at[0]).wait_send()

    def left(k):
        a_copy(me, pal, a_s.at[k]).wait_send()
        a_copy(me, pal, a_f.at[k]).wait_send()
        tc_copy(k).wait_send()
        td_copy(k).wait_send()

    loop(1, nz, left)
    loop(1, n, lambda k: h_copy(row_peer(k), me, k).wait_send())
    ta_copy().wait_send()
    for k in range(1, groups):
        g_copy(k).wait_send()
        tb_copy(k).wait_send()
        c_copy(k).wait_send()
        k_copy(k).wait_send()
        te_copy(k).wait_send()
    for k in range(groups):
        tf_copy(k).wait_send()


def on_device(
    n, groups,
    serving, serving_scale, hot_blocks, bag_lengths, bag_indices, dense_act, labels,
    w_top, w_out, master, accum,
):
    rows, width = serving.shape
    blocks = rows // BLOCK
    count = hot_blocks.shape[1]
    span = count * BLOCK
    bags = bag_lengths.shape[1]
    nnz = bag_indices.shape[1]
    cap = nnz // (2 * n)
    capp = -(-cap // 16) * 16
    feats, ff = w_top.shape
    nz = n // 2
    owned = master.shape[1]
    half_rows = feats * ff // 2 // width
    quarter = half_rows // groups
    piece = quarter // nz
    piece_type = BF if piece % 16 == 0 else F32
    vmem = pl.BlockSpec(memory_space=pltpu.VMEM)
    dma = pltpu.SemaphoreType.DMA
    out = pl.pallas_call(
        functools.partial(kernel, (n, groups, cap)),
        out_shape=(
            jax.ShapeDtypeStruct((owned, width), F32),
            jax.ShapeDtypeStruct((1, owned), F32),
            jax.ShapeDtypeStruct((groups, rows // groups, width), BF),
            jax.ShapeDtypeStruct((1, blocks), BF),
            jax.ShapeDtypeStruct((feats, ff), F32),
        ),
        in_specs=[vmem] * 11,
        out_specs=(vmem,) * 5,
        scratch_shapes=[
            pltpu.VMEM((n, span + 16, width), BF),
            pltpu.VMEM((n, bags, span), BF),
            pltpu.VMEM((n, span, bags), BF),
            pltpu.VMEM((n, capp, span), BF),
            pltpu.VMEM((n, capp + 16, width), BF),
            pltpu.VMEM((n, capp + 16, width), BF),
            pltpu.VMEM((groups, span + 16, width), BF),
            pltpu.VMEM((groups, 16, width), BF),
            pltpu.VMEM((bags, width), F32),
            pltpu.VMEM((bags, feats), BF),
            pltpu.VMEM((2, bags, ff // 2), BF),
            pltpu.VMEM((half_rows, width), BF),
            pltpu.VMEM((half_rows, width), F32),
            pltpu.VMEM((half_rows, width), BF),
            pltpu.VMEM((half_rows, width), BF),
            pltpu.VMEM((groups, quarter, width), BF),
            pltpu.VMEM((nz, piece, width), piece_type),
            pltpu.VMEM((nz, piece, width), piece_type),
            pltpu.VMEM((nz, piece, width), piece_type),
            pltpu.VMEM((groups, quarter, width), BF),
            pltpu.VMEM((groups, quarter, width), BF),
            dma((nz,)), dma((nz,)), dma((n,)),
            dma((n,)), dma((n,)),
            dma((groups,)), dma((groups,)),
            dma((groups,)), dma((groups,)),
            dma((groups,)), dma((groups,)),
            dma, dma,
            dma((groups,)), dma((groups,)),
            dma((nz,)), dma((nz,)),
            dma((nz,)), dma((nz,)),
            dma((groups,)), dma((groups,)),
            dma((groups,)), dma((groups,)),
        ],
        compiler_params=pltpu.CompilerParams(
            collective_id=0, has_side_effects=True, vmem_limit_bytes=60 * 2**20
        ),
        name="step",
    )(
        hot_blocks, serving, serving_scale.reshape(1, -1), bag_lengths, bag_indices, dense_act,
        labels.reshape(1, -1), w_top, w_out.reshape(1, -1), master[0], accum,
    )
    new_master, new_accum, fresh, fresh_scale, top = out
    return (new_master[None], new_accum, fresh.reshape(rows, width), fresh_scale[0], top)


def solution(mesh):
    return jax.shard_map(
        functools.partial(on_device, mesh.shape["row"], mesh.shape["grp"]),
        mesh=mesh,
        in_specs=(
            P("row", None),
            P("row"),
            P("grp", "row"),
            P(("grp", "row"), None),
            P(("grp", "row"), None),
            P(("grp", "row"), None),
            P(("grp", "row")),
            P(),
            P(),
            P("grp", "row", None),
            P("grp", "row"),
        ),
        out_specs=(P("grp", "row", None), P("grp", "row"), P("row", None), P("row"), P()),
        check_vma=False,
    )
```

time: 262 us -> 54.6 us (0.21)
  waiting for transfers between devices: 130 us -> 0 us
  blocking collectives: 65.9 us -> 0 us
  Pallas kernels: 0 us -> 47.4 us
  local copies, waits for them, and re-layouts: 23.5 us -> 6.35 us
  between operations: 17.8 us -> 0.66 us
  other arithmetic: 16 us -> 0 us
  matrix products: 6.17 us -> 0 us
    psum x1 -> x0, waiting for transfers between devices: 115 us -> none  [on_device(): top_grad = lax.psum(top_part, ('grp', 'row'))]
    pallas_call x0 -> x1, Pallas kernels: none -> 47.4 us  [on_device(): pl.pallas_call(functools.partial(kernel, (n, groups, cap)), out_shape=(ja...]
    all_gather x3 -> x0, blocking collectives: 35.6 us -> none  [the longest x1 18.5 us: on_device(): lax.all_gather(picked, 'row', axis=0, tiled=True)]
    unnamed x3 -> x0, blocking collectives: 30.3 us -> none
    gather x4 -> x0, local copies, waits for them, and re-layouts: 18 us -> none  [the longest x2 16.8 us: pool_grad(): indices[positions]]
    reduce_scatter x1 -> x0, waiting for transfers between devices: 14.8 us -> none  [on_device(): lax.psum_scatter(hot_part, 'row', scatter_dimension=0, tiled=True)]
    reduce_sum x1 -> x0, other arithmetic: 10.4 us -> none  [count_block(): jnp.sum((picked[:, :, None] == columns[None, None, :]).astype(jnp.bfloat1...]
    dot_general x6 -> x0, matrix products: 6.17 us -> none  [the longest x1 2.18 us: spread_block(): lax.dot_general(weights, emb_grad, (((0,), (0,)), ((), ())), precision=la...]
  transfers between devices with their start and end apart: 2 -> 0, of which waited for: 2 -> 0; matrix products, arithmetic and copies ran while one was open for 1% -> 0% of each run, Pallas kernels for 0% -> 0%
where the time goes in v1:
time: 54.6 us; the launch traced here: 54.4 us
  Pallas kernels  47.4 us (87%)
  local copies, waits for them, and re-layouts  6.35 us (12%)
  between operations  0.66 us (1%)
    pallas_call x1, Pallas kernels, on_device(): pl.pallas_call(functools.partial(kernel, (n, groups, cap)), out_shape=(ja...  47.4 us
    unnamed x9, local copies, waits for them, and re-layouts  6.35 us

profile of v1, /device:TPU:1, one launch (start us, length us, event | category | flops | bytes accessed | tf_op | source)
XLA Modules:
  0.0 54.4 jit_solution(3094246931563942452)
XLA Ops:
  0.6 47.4 %step.1 = (f32[512,128]{1,0:T(8,128)}, f32[1,512]{1,0:T(1,128)}, bf16[4,512,128]{2,1,0:T(8,128)(2,1)}, bf16[1,16]{1,0:T(2,128)(2,1)}, f32[256,1024]{1,0:T(8,128)}) custom-call(s32[1,2]{1,0:T(1,128)} %hot.1, bf16[2048,128]{1,0:T(8,128)(2,1)} %srv.1, bf16[1,16]{1,0:T(2,128)(2,1)} %bitcast.12, s32[1,256]{1,0:T(1,128)} %lens.1, s32[1,1024]{1,0:T(1,128)} %idx.1, ...), custom_call_target="tpu_custom_call" | custom-call | tf_op jit(solution)/shard_map/step/pallas_call | solution.py:397
  48.0 0.0 copy-start
  48.0 1.8 %copy.21 = f32[1,512,128]{2,1,0:T(8,128)} copy(f32[1,512,128]{2,1,0:T(8,128)} %bitcast.8) | data formatting | bytes 524288
  49.8 1.2 %copy.22 = f32[1,512]{1,0:T(1,128)} copy(f32[1,512]{1,0:T(1,128)} %get-tuple-element.21) | data formatting | bytes 4096
  51.0 0.0 copy-start.1
  51.0 1.9 %copy.23 = bf16[2048,128]{1,0:T(8,128)(2,1)} copy(bf16[2048,128]{1,0:T(8,128)(2,1)} %bitcast.7) | data formatting | bytes 1048576
  52.9 0.0 copy-done.1
  52.9 0.5 copy.24
  53.4 0.0 copy-done
  53.4 1.0 %copy.25 = f32[256,1024]{1,0:T(8,128)} copy(f32[256,1024]{1,0:T(8,128)S(1)} %copy-done) | data formatting | bytes 2097152
Async XLA Ops:
  48.0 5.4 %copy-start = (f32[256,1024]{1,0:T(8,128)S(1)}, f32[256,1024]{1,0:T(8,128)}, u32[]{:S(2)}) copy-start(f32[256,1024]{1,0:T(8,128)} %get-tuple-element.24) | copy-start | bytes 3145732
  51.0 1.9 %copy-start.1 = (bf16[1,16]{1,0:T(2,128)(2,1)S(1)}, bf16[1,16]{1,0:T(2,128)(2,1)}, u32[]{:S(2)}) copy-start(bf16[1,16]{1,0:T(2,128)(2,1)} %get-tuple-element.13) | copy-start | bytes 100

commit v2 on v1

--- a/solution.py
+++ b/solution.py
@@ -50,6 +50,11 @@
 
 
 def loop(lo, hi, body):
+    if hi - lo <= 8:
+        for k in range(lo, hi):
+            body(k)
+        return
+
     def step(k, carry):
         body(k)
         return carry
@@ -61,8 +66,8 @@
     dims,
     hot, srv, scl, lens, idx, dense, labels, w_top, w_out, master, accum,
     o_master, o_accum, o_srv, o_scl, o_top,
-    tbl, cnt, cnt_t, sel, hmsg, hrecv, gbuf, sbuf, pooled, joined, dpre,
-    t_send, t_own, t_a, t_b, t_br, t_c, t_cr, f_d, f_e, f_f,
+    tbl, cnt, few, hmsg, hrecv, gbuf, sbuf, pooled, joined, dpre,
+    t_rows, t_sum, t_send, t_own, t_a, t_b, t_br, t_c, t_cr, f_d, f_e, f_f,
     a_s, a_f, a_r, h_s, h_r, g_s, g_r, c_s, c_r, k_s, k_r,
     ta_s, ta_r, tb_s, tb_r, tc_s, tc_r, td_s, td_r, te_s, te_r, tf_s, tf_r,
 ):
@@ -139,14 +144,14 @@
 
     def count_range(r):
         which = jnp.where(indices - r * span == iota((span, nnz), 0), 1.0, 0.0).astype(BF)
-        cnt_t[r] = nt(which, in_bag).astype(BF)
         counts = nt(in_bag, which)
-        cnt[r] = counts.astype(BF)
+        whole = counts.astype(BF)
+        cnt[r] = whole
         used = jnp.where(jnp.sum(counts, axis=0, keepdims=True) > 0.0, 1.0, 0.0)
         rank = nn(jnp.broadcast_to(used, (8, span)).astype(BF), upper)[0:1, :]
         order = jnp.where(used > 0.0, rank.astype(jnp.int32) - 1, -1)
         picked = jnp.where(iota((width, span), 0) == order, 1.0, 0.0).astype(BF)
-        sel[r] = picked[:capp, :]
+        few[r] = nt(picked[:capp, :], whole).astype(BF)
         hmsg[r, capp:capp + 16, :] = jnp.concatenate(
             [nt(numbers, picked), jnp.zeros((8, width), F32)], axis=0
         ).astype(BF)
@@ -154,20 +159,6 @@
     loop(0, n, count_range)
 
     joined[:, width:] = dense[...]
-
-    def relay(k):
-        source = chip_peer(k)
-        a_copy(source, source, a_f.at[k]).wait_recv()
-        a_copy(source, pal, a_f.at[k]).start()
-
-    loop(1, nz, relay)
-
-    def other(k):
-        source = ((z + k) % nz) * 2 + (1 - c)
-        a_copy(source, pal, a_f.at[0]).wait_recv()
-
-    loop(0, nz, other)
-    pooled[...] = jnp.zeros_like(pooled)
 
     def pool(r):
         block_scale = tbl[r, span:span + 16, :].astype(F32)
@@ -177,7 +168,23 @@
             total = total + nn(cnt[r, :, part], tbl[r, part, :]) * block_scale[j:j + 1, :]
         pooled[...] = total
 
-    loop(0, n, pool)
+    pooled[...] = jnp.zeros_like(pooled)
+    pool(me)
+
+    def relay(k):
+        source = chip_peer(k)
+        a_copy(source, source, a_f.at[k]).wait_recv()
+        a_copy(source, pal, a_f.at[k]).start()
+        pool(source)
+
+    loop(1, nz, relay)
+
+    def other(k):
+        source = ((z + k) % nz) * 2 + (1 - c)
+        a_copy(source, pal, a_f.at[0]).wait_recv()
+        pool(source)
+
+    loop(0, nz, other)
     joined[:, :width] = pooled[...].astype(BF)
 
     pre = nn(joined[...], w_top[...])
@@ -190,17 +197,6 @@
     dpre[1] = dp[:, half:]
     dz = nt(dp, w_top[:width, :]).astype(BF)
 
-    def h_copy(to, source, k):
-        return rcopy(hmsg.at[to], hrecv.at[source], h_s.at[k], h_r.at[source], (g, to))
-
-    def spread(k):
-        to = row_peer(k)
-        rows = nn(cnt_t[to], dz).astype(BF)
-        hmsg[to, :capp, :] = nn(sel[to], rows).astype(BF)
-        h_copy(to, me, k).start()
-
-    loop(1, n, spread)
-
     def ta_copy():
         return rcopy(t_send, t_a, ta_s, ta_r, (g, pal))
 
@@ -209,29 +205,19 @@
     for j in range(half // BLOCK):
         t_send[j * feats:(j + 1) * feats, :] = theirs[:, j * BLOCK:(j + 1) * BLOCK].astype(BF)
     ta_copy().start()
+
+    def h_copy(to, source, k):
+        return rcopy(hmsg.at[to], hrecv.at[source], h_s.at[k], h_r.at[source], (g, to))
+
+    def spread(r):
+        hmsg[r, :capp, :] = nn(few[r], dz).astype(BF)
+
+    loop(0, n, spread)
+    loop(1, n, lambda k: h_copy(row_peer(k), me, k).start())
+
     mine = tn(joined[...], dpre[c])
     for j in range(half // BLOCK):
         t_own[j * feats:(j + 1) * feats, :] = mine[:, j * BLOCK:(j + 1) * BLOCK]
-
-    pooled[...] = jnp.zeros_like(pooled)
-    t_rows = nn(cnt_t[me], dz)
-
-    def g_copy(k):
-        return rcopy(gbuf.at[g], gbuf.at[g], g_s.at[k], g_r.at[k], (grp_peer(k), me))
-
-    def arrive(k, total):
-        source = row_peer(k)
-        h_copy(source, source, k).wait_recv()
-        place_of = hrecv[source, capp:capp + 1, :].astype(F32)
-        put = jnp.where(
-            iota((span, width), 0).astype(F32) == place_of, 1.0, 0.0
-        ).astype(BF)
-        return total + nn(put[:, :capp], hrecv[source, :capp, :])
-
-    summed = lax.fori_loop(1, n, arrive, t_rows)
-    gbuf[g, :span, :] = summed.astype(BF)
-    for k in range(1, groups):
-        g_copy(k).start()
 
     quarter = t_own.shape[0] // groups
 
@@ -249,6 +235,55 @@
     t_b[...] = both.astype(BF)
     for k in range(1, groups):
         tb_copy(k).start()
+
+    def g_copy(k):
+        return rcopy(gbuf.at[g], gbuf.at[g], g_s.at[k], g_r.at[k], (grp_peer(k), me))
+
+    def expand(message):
+        place_of = message[capp:capp + 1, :].astype(F32)
+        put = jnp.where(
+            iota((span, width), 0).astype(F32) == place_of, 1.0, 0.0
+        ).astype(BF)
+        return nn(put[:, :capp], message[:capp, :])
+
+    t_rows[...] = expand(hmsg[me])
+
+    def arrive(k):
+        source = row_peer(k)
+        h_copy(source, source, k).wait_recv()
+        t_rows[...] += expand(hrecv[source])
+
+    loop(1, n, arrive)
+    gbuf[g, :span, :] = t_rows[...].astype(BF)
+    for k in range(1, groups):
+        g_copy(k).start()
+
+    def tc_copy(k):
+        to = chip_peer(k)
+        return rcopy(t_c.at[to // 2], t_cr.at[k], tc_s.at[k], tc_r.at[k], (g, to))
+
+    total = t_own[pl.ds(pl.multiple_of(g * quarter, quarter), quarter), :]
+    for k in range(1, groups):
+        tb_copy(k).wait_recv()
+        total = total + t_br[k].astype(F32)
+    piece = quarter // nz
+    for q in range(nz):
+        t_c[q] = total[q * piece:(q + 1) * piece, :].astype(t_c.dtype)
+    loop(1, nz, lambda k: tc_copy(k).start())
+
+    t_sum[...] = t_c[z].astype(F32)
+
+    def gather_piece(k):
+        tc_copy(k).wait_recv()
+        t_sum[...] += t_cr[k].astype(F32)
+
+    loop(1, nz, gather_piece)
+
+    def td_copy(k):
+        return rcopy(f_d.at[z], f_d.at[z], td_s.at[k], td_r.at[k], (g, chip_peer(k)))
+
+    f_d[z] = t_sum[...].astype(BF).astype(f_d.dtype)
+    loop(1, nz, lambda k: td_copy(k).start())
 
     for k in range(1, groups):
         g_copy(k).wait_recv()
@@ -285,30 +320,6 @@
         c_copy(k).start()
         k_copy(k).start()
 
-    def tc_copy(k):
-        to = chip_peer(k)
-        return rcopy(t_c.at[to // 2], t_cr.at[k], tc_s.at[k], tc_r.at[k], (g, to))
-
-    total = t_own[pl.ds(pl.multiple_of(g * quarter, quarter), quarter), :]
-    for k in range(1, groups):
-        tb_copy(k).wait_recv()
-        total = total + t_br[k].astype(F32)
-    piece = quarter // nz
-    for q in range(nz):
-        t_c[q] = total[q * piece:(q + 1) * piece, :].astype(t_c.dtype)
-    loop(1, nz, lambda k: tc_copy(k).start())
-
-    def gather_piece(k, total):
-        tc_copy(k).wait_recv()
-        return total + t_cr[k].astype(F32)
-
-    final = lax.fori_loop(1, nz, gather_piece, t_c[z].astype(F32))
-
-    def td_copy(k):
-        return rcopy(f_d.at[z], f_d.at[z], td_s.at[k], td_r.at[k], (g, chip_peer(k)))
-
-    f_d[z] = final.astype(BF).astype(f_d.dtype)
-    loop(1, nz, lambda k: td_copy(k).start())
     loop(1, nz, lambda k: td_copy(k).wait_recv())
 
     def te_copy(k):
@@ -339,12 +350,13 @@
     o_scl[...] = line[:, :groups * per].astype(BF)
 
     def place_half(ref, at):
-        flat = ref[...].reshape(groups * quarter, width).astype(F32)
+        flat = ref[...].reshape(groups * quarter, width)
         for j in range(half // BLOCK):
             column = pl.multiple_of(at * half + j * BLOCK, BLOCK)
             o_top[:, pl.ds(column, BLOCK)] = flat[j * feats:(j + 1) * feats, :]
 
     place_half(f_e, c)
+
     for k in range(groups):
         tf_copy(k).wait_recv()
     place_half(f_f, 1 - c)
@@ -370,6 +382,11 @@
         te_copy(k).wait_send()
     for k in range(groups):
         tf_copy(k).wait_send()
+
+
+def write_out(*refs):
+    for source, target in zip(refs[:5], refs[5:]):
+        target[...] = source[...].astype(target.dtype)
 
 
 def on_device(
@@ -401,15 +418,14 @@
             jax.ShapeDtypeStruct((1, owned), F32),
             jax.ShapeDtypeStruct((groups, rows // groups, width), BF),
             jax.ShapeDtypeStruct((1, blocks), BF),
-            jax.ShapeDtypeStruct((feats, ff), F32),
+            jax.ShapeDtypeStruct((feats, ff), BF),
         ),
         in_specs=[vmem] * 11,
         out_specs=(vmem,) * 5,
         scratch_shapes=[
             pltpu.VMEM((n, span + 16, width), BF),
             pltpu.VMEM((n, bags, span), BF),
-            pltpu.VMEM((n, span, bags), BF),
-            pltpu.VMEM((n, capp, span), BF),
+            pltpu.VMEM((n, capp, bags), BF),
             pltpu.VMEM((n, capp + 16, width), BF),
             pltpu.VMEM((n, capp + 16, width), BF),
             pltpu.VMEM((groups, span + 16, width), BF),
@@ -417,6 +433,8 @@
             pltpu.VMEM((bags, width), F32),
             pltpu.VMEM((bags, feats), BF),
             pltpu.VMEM((2, bags, ff // 2), BF),
+            pltpu.VMEM((span, width), F32),
+            pltpu.VMEM((piece, width), F32),
             pltpu.VMEM((half_rows, width), BF),
             pltpu.VMEM((half_rows, width), F32),
             pltpu.VMEM((half_rows, width), BF),
@@ -447,8 +465,20 @@
         hot_blocks, serving, serving_scale.reshape(1, -1), bag_lengths, bag_indices, dense_act,
         labels.reshape(1, -1), w_top, w_out.reshape(1, -1), master[0], accum,
     )
-    new_master, new_accum, fresh, fresh_scale, top = out
-    return (new_master[None], new_accum, fresh.reshape(rows, width), fresh_scale[0], top)
+    new_master, new_accum, fresh, fresh_scale, top = pl.pallas_call(
+        write_out,
+        out_shape=(
+            jax.ShapeDtypeStruct((owned, width), F32),
+            jax.ShapeDtypeStruct((1, owned), F32),
+            jax.ShapeDtypeStruct((rows, width), BF),
+            jax.ShapeDtypeStruct((1, blocks), BF),
+            jax.ShapeDtypeStruct((feats, ff), F32),
+        ),
+        in_specs=[vmem] * 5,
+        out_specs=(vmem,) * 5,
+        name="write",
+    )(out[0], out[1], out[2].reshape(rows, width), out[3], out[4])
+    return (new_master[None], new_accum, fresh, fresh_scale[0], top)
 
 
 def solution(mesh):

time: 54.6 us -> 43.9 us (0.80)
  local copies, waits for them, and re-layouts: 6.35 us -> 0 us
  Pallas kernels: 47.4 us -> 43.1 us
    pallas_call x1, Pallas kernels: 47.4 us -> 40.5 us  [on_device(): pl.pallas_call(functools.partial(kernel, (n, groups, cap)), out_shape=(ja...]
    unnamed x9 -> x0, local copies, waits for them, and re-layouts: 6.35 us -> none
    pallas_call x0 -> x1, Pallas kernels: none -> 2.54 us  [on_device(): pl.pallas_call(write_out, out_shape=(jax.ShapeDtypeStruct((owned, width),...]
where the time goes in v2:
time: 43.9 us; the launch traced here: 43.7 us
  Pallas kernels  43.1 us (98%)
  between operations  0.64 us (1%)
    pallas_call x1, Pallas kernels, on_device(): pl.pallas_call(functools.partial(kernel, (n, groups, cap)), out_shape=(ja...  40.5 us
    pallas_call x1, Pallas kernels, on_device(): pl.pallas_call(write_out, out_shape=(jax.ShapeDtypeStruct((owned, width),...  2.54 us

profile of v2, /device:TPU:1, one launch (start us, length us, event | category | flops | bytes accessed | tf_op | source)
XLA Modules:
  0.0 43.7 jit_solution(9462289112713426915)
XLA Ops:
  0.6 40.5 %step.1 = (f32[512,128]{1,0:T(8,128)}, f32[1,512]{1,0:T(1,128)}, bf16[4,512,128]{2,1,0:T(8,128)(2,1)}, bf16[1,16]{1,0:T(2,128)(2,1)}, bf16[256,1024]{1,0:T(8,128)(2,1)}) custom-call(s32[1,2]{1,0:T(1,128)} %hot.1, bf16[2048,128]{1,0:T(8,128)(2,1)} %srv.1, bf16[1,16]{1,0:T(2,128)(2,1)} %bitcast.11, s32[1,256]{1,0:T(1,128)} %lens.1, s32[1,1024]{1,0:T(1,128)} %idx.1, ...), custom_call_target="tpu_custom_call" | custom-call | tf_op jit(solution)/shard_map/step/pallas_call | solution.py:414
  41.2 2.5 %write.1 = (f32[512,128]{1,0:T(8,128)}, f32[1,512]{1,0:T(1,128)}, bf16[2048,128]{1,0:T(8,128)(2,1)}, bf16[1,16]{1,0:T(2,128)(2,1)}, f32[256,1024]{1,0:T(8,128)}) custom-call(f32[512,128]{1,0:T(8,128)} %get-tuple-element.15.refs_0_, f32[1,512]{1,0:T(1,128)} %get-tuple-element.16.refs_1_, bf16[2048,128]{1,0:T(8,128)(2,1)} %bitcast.7, ...), custom_call_target="tpu_custom_call" | custom-call | tf_op jit(solution)/shard_map/write/pallas_call | solution.py:468
